TPU v7x, 128 devices: a whole 4x4x4 slice. The times are simulated.
128 devices in a mesh: dp: 64 (over z, y, x), tensor: 2 (over core).
Axes of the slice: x: 4, y: 4, z: 4, core: 2. Of those that a mesh axis runs over, the one named last changes fastest.
Arguments:
- current: float32 [128, 4096], P('dp'), may hold values from -6 to 6
- noise_draw: float32 [128, 4096], P('dp'), may hold values from -6 to 6
- labels: bfloat16 [128, 1152], P('dp'), may hold values from -6 to 6
- time_now: float32 [128], P('dp'), may hold values from 0.4 to 1
- step_size: float32 [128], P('dp'), may hold values from 0.005 to 0.02
- accept: int32 [128], P('dp'), may hold values 0 or 1
- patch_weight: bfloat16 [16, 1152], replicated, may hold values from -1.5 to 1.5
- time_in: bfloat16 [256, 1152], replicated, may hold values from -0.375 to 0.375
- time_out: bfloat16 [1152, 1152], replicated, may hold values from -0.1875 to 0.1875
- qkv_weight: bfloat16 [1, 1152, 3, 1152], P(None, None, None, 'tensor'), may hold values from -1 to 1
- out_weight: bfloat16 [1, 1152, 1152], P(None, None, 'tensor'), may hold values from -0.1875 to 0.1875
- ada_weight: bfloat16 [1, 1152, 3456], P(None, 'dp', 'tensor'), may hold values from -0.1875 to 0.1875
- final_ada: bfloat16 [1152, 2304], P('dp', 'tensor'), may hold values from -0.1875 to 0.1875
- final_proj: bfloat16 [1152, 16], replicated, may hold values from -0.1875 to 0.1875
Outputs:
- next_state: float32 [128, 4096], P('dp')
- error_norm: float32 [128], P('dp')
All inputs are finite; a program needn't handle non-finite values. No bound on the sum of `accept` on one device may be relied on, other than what follows from the above.
Results may differ from a plain program's by a relative error of at most 0.015.
Values may be sent and summed in bfloat16 or wider, within the bound.
A program may use at most 128 MiB of HBM per device.

v0:
```python
import math
import jax
import jax.numpy as jnp
from jax import lax
from jax.sharding import PartitionSpec as P

D = 1152
PATCH_VALS = 16
HEAD_DIM = 72
beta_low = 0.1
beta_high = 20.0
tol_abs = 0.0078
tol_rel = 0.05
norm_eps = 1e-06


def from_everyone(array, axis):
    peers = lax.axis_size(axis)
    return lax.all_to_all(
        jnp.broadcast_to(array[None], (peers, *array.shape)), axis, 0, 0, tiled=True
    )


def of_everyone(array, axis):
    return from_everyone(array, axis).astype(jnp.float32).sum(axis=0)


def beta_at(moments):
    return beta_low + (beta_high - beta_low) * moments


def sigma_at(moments):
    integral = beta_low * moments + 0.5 * (beta_high - beta_low) * moments * moments
    return jnp.sqrt(1.0 - jnp.exp(-integral))


def time_features(moments, feature_count):
    half_count = feature_count // 2
    freq_index = jnp.arange(half_count, dtype=jnp.float32)
    freq_rates = jnp.exp(-math.log(10000.0) * freq_index / half_count)
    angles = 1000.0 * moments[:, None] * freq_rates[None, :]
    return jnp.concatenate([jnp.cos(angles), jnp.sin(angles)], axis=1)


def position_table(positions, feature_count):
    half_count = feature_count // 2
    freq_index = jnp.arange(half_count, dtype=jnp.float32)
    freq_rates = jnp.exp(-math.log(10000.0) * freq_index / half_count)
    angles = positions.astype(jnp.float32)[:, None] * freq_rates[None, :]
    return jnp.concatenate([jnp.sin(angles), jnp.cos(angles)], axis=1)


def condition(moments, labels, time_in, time_out):
    features = time_features(moments, time_in.shape[0]).astype(jnp.bfloat16)
    hidden = jax.nn.silu(jnp.dot(features, time_in, preferred_element_type=jnp.float32)).astype(
        jnp.bfloat16
    )
    joined = labels.astype(jnp.float32) + jnp.dot(
        hidden, time_out, preferred_element_type=jnp.float32
    )
    return jax.nn.silu(joined).astype(jnp.bfloat16)


def layer_norm(values):
    average = jnp.mean(values, axis=-1, keepdims=True)
    centred = values - average
    spread_sq = jnp.mean(centred * centred, axis=-1, keepdims=True)
    return centred * lax.rsqrt(spread_sq + norm_eps)


def modulate(values, shift_vec, scale_vec):
    return (layer_norm(values) * (1.0 + scale_vec[:, None]) + shift_vec[:, None]).astype(
        jnp.bfloat16
    )


def drift(values, moments, noise_guess):
    beta_rate = beta_at(moments)[:, None]
    return 0.5 * beta_rate * values - beta_rate * noise_guess / sigma_at(moments)[:, None]


def attend(projected, head_dim):
    lat_count, token_count, _, feature_width = projected.shape
    head_count = feature_width // head_dim
    shaped = projected.reshape(lat_count, token_count, 3, head_count, head_dim)
    scores = jnp.einsum(
        "lqhe,lkhe->lhqk", shaped[:, :, 0], shaped[:, :, 1], preferred_element_type=jnp.float32
    ) * head_dim ** (-0.5)
    attn_probs = jax.nn.softmax(scores, axis=-1).astype(jnp.bfloat16)
    mixture = jnp.einsum(
        "lhqk,lkhe->lqhe", attn_probs, shaped[:, :, 2], preferred_element_type=jnp.float32
    )
    return mixture.astype(jnp.bfloat16).reshape(lat_count, token_count, feature_width)


def shards(
    current,
    noise_draw,
    labels,
    time_now,
    step_size,
    accept,
    patch_weight,
    time_in,
    time_out,
    qkv_weight,
    out_weight,
    ada_weight,
    final_ada,
    final_proj,
):
    lat_count = current.shape[0]
    tok_count = current.shape[1] // PATCH_VALS
    layer_total = ada_weight.shape[0]
    layer_cols = ada_weight.shape[2]
    final_cols = final_ada.shape[1]
    tensor_size = lax.axis_size("tensor")
    later_time = time_now - step_size
    moments = jnp.concatenate([time_now, later_time])
    cond_act = condition(moments, jnp.concatenate([labels, labels], axis=0), time_in, time_out)
    own_rows = ada_weight.shape[1]
    packed = jnp.concatenate(
        [ada_weight.transpose(1, 0, 2).reshape(own_rows, layer_total * layer_cols), final_ada],
        axis=1,
    )
    row_total = cond_act.shape[0]
    packed_width = packed.shape[1]
    mod_local = jnp.dot(
        cond_act,
        lax.all_gather(packed, "dp", axis=0, tiled=True),
        preferred_element_type=jnp.float32,
    )
    gathered = lax.all_gather(mod_local.astype(jnp.bfloat16), "tensor", axis=1, tiled=True).astype(
        mod_local.dtype
    )
    arranged = gathered.reshape(row_total, tensor_size, packed_width)
    layer_mods = arranged[:, :, : layer_total * layer_cols].reshape(
        row_total, tensor_size, layer_total, layer_cols
    )
    layer_mods = layer_mods.transpose(0, 2, 1, 3).reshape(
        row_total, layer_total, tensor_size * layer_cols
    )
    final_mods = arranged[:, :, layer_total * layer_cols :].reshape(
        row_total, tensor_size * final_cols
    )
    positions = position_table(jnp.arange(tok_count, dtype=jnp.int32), D)

    def evaluate(latents, mod_rows, final_rows):
        tokens = latents.reshape(lat_count, tok_count, PATCH_VALS).astype(jnp.bfloat16)
        stream = (
            jnp.einsum("ltc,cd->ltd", tokens, patch_weight, preferred_element_type=jnp.float32)
            + positions[None]
        )
        shift_attn, scale_attn, gate_attn = jnp.split(mod_rows[:, 0], 3, axis=1)
        attn_in = modulate(stream, shift_attn, scale_attn)
        projected = jnp.einsum(
            "ltd,dck->ltck", attn_in, qkv_weight[0], preferred_element_type=jnp.float32
        ).astype(jnp.bfloat16)
        attended = attend(projected, HEAD_DIM)
        partial_value = jnp.einsum(
            "ltk,dk->ltd", attended, out_weight[0], preferred_element_type=jnp.float32
        )
        attn_sum = of_everyone(partial_value.astype(jnp.bfloat16), "tensor").astype(jnp.float32)
        stream = stream + gate_attn[:, None] * attn_sum
        shift_final, scale_final = jnp.split(final_rows, 2, axis=1)
        final_in = modulate(stream, shift_final, scale_final)
        guessed = jnp.einsum(
            "ltd,dc->ltc", final_in, final_proj, preferred_element_type=jnp.float32
        )
        return guessed.reshape(lat_count, tok_count * PATCH_VALS)

    noise_now = evaluate(current, layer_mods[:lat_count], final_mods[:lat_count])
    drift_now = drift(current, time_now, noise_now)
    spread = jnp.sqrt(step_size * beta_at(time_now))[:, None] * noise_draw
    euler_state = current + step_size[:, None] * drift_now + spread
    noise_later = evaluate(euler_state, layer_mods[lat_count:], final_mods[lat_count:])
    drift_later = drift(euler_state, later_time, noise_later)
    heun_state = current + 0.5 * step_size[:, None] * (drift_now + drift_later) + spread
    scale_ref = jnp.maximum(tol_abs, tol_rel * jnp.maximum(jnp.abs(heun_state), jnp.abs(current)))
    scaled_gap = (euler_state - heun_state) / scale_ref
    error_norm = jnp.sqrt(jnp.sum(scaled_gap * scaled_gap, axis=1) / current.shape[1])
    next_state = jnp.where(accept[:, None] == 1, heun_state, current)
    return (next_state, error_norm)


def solution(mesh):
    in_specs = (
        P("dp", None),
        P("dp", None),
        P("dp", None),
        P("dp"),
        P("dp"),
        P("dp"),
        P(),
        P(),
        P(),
        P(None, None, None, "tensor"),
        P(None, None, "tensor"),
        P(None, "dp", "tensor"),
        P("dp", "tensor"),
        P(),
    )
    out_specs = (P("dp", None), P("dp"))
    return jax.shard_map(shards, mesh=mesh, in_specs=in_specs, out_specs=out_specs, check_vma=False)
```

profile of v0, /device:TPU:1, one launch (start us, length us, event | category | flops | bytes accessed | tf_op | source)
XLA Modules:
  0.0 162.8 jit_solution(1953090648457118049)
XLA Ops:
  7.2 1.8 %maximum_bitcast_fusion = bf16[1,18,2880]{2,1,0:T(8,128)(2,1)} fusion(bf16[18,1152]{1,0:T(8,128)(2,1)} %param.26, bf16[18,1728]{1,0:T(8,128)(2,1)} %bitcast.106), kind=kLoop, calls=%fused_computation.66 | loop fusion | flops 207360 | bytes 207360
  9.1 0.8 convert_element_type.83
  10.0 0.7 broadcast_multiply_fusion.4
  10.7 0.7 maximum_multiply_fusion
  11.4 2.3 %multiply_sine_fusion = (f32[256,576]{1,0:T(8,128)S(1)}, f32[256,576]{1,0:T(8,128)S(1)}) fusion(f32[576]{0:T(1024)S(1)} %multiply_exponential_fusion, f32[256]{0:T(256)S(1)} %iota_convert_fusion), kind=kLoop, calls=%fused_computation.57 | loop fusion | flops 147456 | bytes 1182976 | tf_op jit(solution)/shard_map/sin | solution.py:50
  13.8 0.2 pad_maximum_fusion
  14.1 1.0 copy-done.4
  15.1 0.5 fusion.78
  15.6 1.4 copy-done.2
  17.0 0.4 multiply_reduce_fusion.5
  17.5 0.2 fusion.60
  17.7 76.3 %all-gather.4.cloned.1.call-done = bf16[64,18,2880]{2,1,0:T(8,128)(2,1)} async-done(((bf16[1,18,2880]{2,1,0:T(8,128)(2,1)}), bf16[64,18,2880]{2,1,0:T(8,128)(2,1)}) %all-gather.4.cloned.1.call-update) | async-done | bytes 6635536 | tf_op jit(solution)/shard_map/all_gather | solution.py:130
  94.0 10.0 %reshape.163 = bf16[1152,2880]{1,0:T(8,128)(2,1)} reshape(bf16[64,18,2880]{2,1,0:T(8,128)(2,1)} %all-gather.4.cloned.1.call-done) | data formatting | bytes 13271040
  104.1 4.3 %fusion.8 = bf16[1,2880,4]{1,2,0:T(4,128)(2,1)S(1)} fusion(bf16[1152,2880]{1,0:T(8,128)(2,1)} %reshape.163, bf16[1152,1152]{1,0:T(8,128)(2,1)S(1)} %copy-done, f32[4,1152]{1,0:T(4,128)S(1)} %fusion.60, bf16[2,1152]{1,0:T(2,128)(2,1)S(1)} %copy-done.9), kind=kOutput, calls=%fused_computation.19 | convolution fusion | flops 37239552 | bytes 9335808 | tf_op jit(solution)/shard_map/dot_general | solution.py:128
  108.4 2.3 %all-gather.1 = bf16[2,2880,4]{1,2,0:T(4,128)(2,1)S(1)} all-gather(bf16[1,2880,4]{1,2,0:T(4,128)(2,1)S(1)} %fusion.8), channel_id=1, replica_groups=mesh['dp'=64,'tensor'=2] {'tensor'}, dimensions={0}, use_global_device_ids=true | all-gather | bytes 69120 | tf_op jit(solution)/shard_map/all_gather | solution.py:133
  111.3 5.6 %fusion.17 = bf16[2,256,3,576]{1,3,2,0:T(8,128)(2,1)S(1)} fusion(bf16[1,1152,3,576]{1,3,2,0:T(8,128)(2,1)} %param.23, f32[2,256,1152]{2,1,0:T(8,128)} %copy-done.2, f32[2,1152]{1,0:T(2,128)S(1)} %get-tuple-element.21, f32[2,1152]{1,0:T(2,128)S(1)} %get-tuple-element.22, f32[2,256]{1,0:T(2,128)S(1)} %add_rsqrt_fusion.3, ...), kind=kOutput, calls=%fused_computation.37 | convolution fusion | flops 2042265600 | bytes 8132608 | tf_op jit(solution)/shard_map/ltd,dck->ltck/dot_general | solution.py:156
  116.8 0.7 fusion.42
  117.6 3.2 %fusion.79 = (f32[2,8,256]{2,1,0:T(8,128)S(1)}, f32[2,8,256,256]{2,3,1,0:T(8,128)S(1)}) fusion(f32[2,8,256,256]{2,3,1,0:T(8,128)S(1)} %fusion.42), kind=kOutput, calls=%fused_computation.139 | output fusion | flops 4194559 | bytes 8404992 | tf_op jit(solution)/shard_map/sub | solution.py:89
  120.8 0.5 fusion.26
  121.4 0.8 copy-done.11
  122.2 1.2 convolution_convert_fusion.2
  123.4 0.2 broadcast_in_dim.10
  123.5 5.7 %all_to_all.10 = bf16[2,2,256,1152]{3,2,1,0:T(8,128)(2,1)S(1)} all-to-all(bf16[2,2,256,1152]{3,2,1,0:T(8,128)(2,1)S(1)} %broadcast_in_dim.10), channel_id=1, replica_groups=mesh['dp'=64,'tensor'=2] {'tensor'}, dimensions={0} | all-to-all | bytes 4718592 | tf_op jit(solution)/shard_map/all_to_all | solution.py:19
  129.2 0.4 convert_reduce_fusion.1
  129.6 1.3 copy-done.3
  130.9 0.3 fusion.74
  131.3 0.4 multiply_reduce_fusion.4
  131.7 0.3 copy-done.13
  132.0 0.6 fusion.39
  132.6 0.2 reshape.156
  133.0 1.8 %fusion.80 = (f32[2,256]{1,0:T(2,128)S(1)}, f32[2,256,1152]{2,1,0:T(8,128)S(1)}) fusion(f32[256,1152]{1,0:T(8,128)} %copy-done.4, bf16[2,256,16]{2,1,0:T(8,128)(2,1)S(1)} %convert_element_type.99, bf16[16,1152]{1,0:T(8,128)(2,1)S(1)} %copy-done.7), kind=kOutput, calls=%fused_computation.140 | convolution fusion | flops 20053504 | bytes 3594240 | tf_op jit(solution)/shard_map/ltc,cd->ltd/dot_general | solution.py:151
  134.8 0.4 multiply_reduce_fusion.3
  135.4 4.8 %fusion.20 = bf16[2,256,3,576]{1,3,2,0:T(8,128)(2,1)S(1)} fusion(bf16[1,1152,3,576]{1,3,2,0:T(8,128)(2,1)} %param.23, f32[2,256,1152]{2,1,0:T(8,128)S(1)} %get-tuple-element.43, f32[2,1152]{1,0:T(2,128)S(1)} %get-tuple-element.18, f32[2,1152]{1,0:T(2,128)S(1)} %get-tuple-element.19, f32[2,256]{1,0:T(2,128)S(1)} %add_rsqrt_fusion.1, ...), kind=kOutput, calls=%fused_computation.38 | convolution fusion | flops 2042265600 | bytes 8132608 | tf_op jit(solution)/shard_map/ltd,dck->ltck/dot_general | solution.py:156
  140.2 0.7 fusion.41
  141.0 3.2 %fusion.81 = (f32[2,8,256]{2,1,0:T(8,128)S(1)}, f32[2,8,256,256]{2,3,1,0:T(8,128)S(1)}) fusion(f32[2,8,256,256]{2,3,1,0:T(8,128)S(1)} %fusion.41), kind=kOutput, calls=%fused_computation.141 | output fusion | flops 4194559 | bytes 8404992 | tf_op jit(solution)/shard_map/sub | solution.py:89
  144.2 0.5 fusion.25
  144.7 0.8 copy-done.12
  145.5 1.2 convolution_convert_fusion.1
  146.7 0.2 broadcast_in_dim.11
  146.9 5.6 %all_to_all.11 = bf16[2,2,256,1152]{3,2,1,0:T(8,128)(2,1)S(1)} all-to-all(bf16[2,2,256,1152]{3,2,1,0:T(8,128)(2,1)S(1)} %broadcast_in_dim.11), channel_id=1, replica_groups=mesh['dp'=64,'tensor'=2] {'tensor'}, dimensions={0} | all-to-all | bytes 4718592 | tf_op jit(solution)/shard_map/all_to_all | solution.py:19
  152.5 0.4 convert_reduce_fusion
  152.9 0.4 fusion.72
  153.3 0.4 multiply_reduce_fusion.2
  153.7 0.6 fusion.40
  154.3 0.2 reshape.159
  154.5 0.3 multiply_reduce_fusion.6
  154.8 0.5 multiply_sqrt_fusion
  155.3 0.7 broadcast_select_fusion
  (56 shorter events, 1.4 us)
Async XLA Ops:
  7.2 96.9 %copy-start = (bf16[1152,1152]{1,0:T(8,128)(2,1)S(1)}, bf16[1152,1152]{1,0:T(8,128)(2,1)}, u32[]{:S(2)}) copy-start(bf16[1152,1152]{1,0:T(8,128)(2,1)} %param.22) | copy-start | bytes 7962628
  7.2 7.9 %copy-start.7 = (bf16[16,1152]{1,0:T(8,128)(2,1)S(1)}, bf16[16,1152]{1,0:T(8,128)(2,1)}, u32[]{:S(2)}) copy-start(bf16[16,1152]{1,0:T(8,128)(2,1)} %param.20) | copy-start | bytes 110596
  7.2 86.8 %all-gather.4.cloned.1.call-start = ((), (), s32[]{:S(2)}) async-start(), calls=%async_computation.2 | async-start | bytes 9185280 | tf_op jit(solution)/shard_map/all_gather | solution.py:130
  14.0 1.0 copy-start.4
  15.1 2.3 %copy-start.14 = (s32[2]{0:T(128)S(1)}, s32[2]{0:T(128)}, u32[]{:S(2)}) copy-start(s32[2]{0:T(128)} %param.19) | copy-start | bytes 28
  15.1 2.5 %copy-start.5 = (bf16[256,1152]{1,0:T(8,128)(2,1)S(1)}, bf16[256,1152]{1,0:T(8,128)(2,1)}, u32[]{:S(2)}) copy-start(bf16[256,1152]{1,0:T(8,128)(2,1)} %param.21) | copy-start | bytes 1769476
  15.6 1.4 copy-start.2
  17.7 86.3 %copy-start.9 = (bf16[2,1152]{1,0:T(2,128)(2,1)S(1)}, bf16[2,1152]{1,0:T(2,128)(2,1)}, u32[]{:S(2)}) copy-start(bf16[2,1152]{1,0:T(2,128)(2,1)} %param.16) | copy-start | bytes 13828
  120.8 1.3 copy-start.11
  129.2 1.7 %copy-start.3 = (f32[2,256,1152]{2,1,0:T(8,128)S(1)}, f32[2,256,1152]{2,1,0:T(8,128)}, u32[]{:S(2)}) copy-start(f32[2,256,1152]{2,1,0:T(8,128)} %copy-done.2) | copy-start | bytes 7077892
  131.2 0.8 copy-start.13
  131.6 1.1 copy-start.6
  131.6 1.1 copy-start.8
  131.6 1.1 copy-start.10
  144.2 1.3 copy-start.12
  153.3 2.7 %copy-start.1 = (bf16[1152,1152]{1,0:T(8,128)(2,1)S(1)}, bf16[1152,1152]{1,0:T(8,128)(2,1)}, u32[]{:S(2)}) copy-start(bf16[1152,1152]{1,0:T(8,128)(2,1)} %param.22) | copy-start | bytes 7962628
Sparse Core Ops, SparseCore 0:
  10.9 83.1 all-gather.3
where the time goes:
time: 164 us; the launch traced here: 163 us
  waiting for transfers between devices  76.3 us (47%)
  matrix products  23.3 us (14%)
  other arithmetic  17.9 us (11%)
  local copies, waits for them, and re-layouts  17.2 us (10%)
  between operations  14.5 us (9%)
  blocking collectives  13.6 us (8%)
    all_gather x1, waiting for transfers between devices, shards(): lax.all_gather(packed, 'dp', axis=0, tiled=True)  76.3 us
    unnamed x34, local copies, waits for them, and re-layouts  15.8 us
    all_to_all x2, blocking collectives, from_everyone(): lax.all_to_all(jnp.broadcast_to(array[None], (peers, *array.shape)), axis...  11.2 us
    dot_general x2, matrix products, evaluate(): jnp.einsum('ltd,dck->ltck', attn_in, qkv_weight[0], preferred_element_typ...  10.4 us
    sub x2, other arithmetic, attend(): attn_probs = jax.nn.softmax(scores, axis=-1).astype(jnp.bfloat16)  6.48 us
    dot_general x1, matrix products, shards(): jnp.dot(cond_act, lax.all_gather(packed, 'dp', axis=0, tiled=True), prefe...  4.3 us
  transfers between devices with their start and end apart: 1, of which 1 were waited for; matrix products, arithmetic and copies ran while one was open for 4% of the time, Pallas kernels for 0%

commit v1 on v0

--- a/solution.py
+++ b/solution.py
@@ -12,6 +12,12 @@
 tol_abs = 0.0078
 tol_rel = 0.05
 norm_eps = 1e-06
+
+
+def gather_from_all(x, axis, dim):
+    devices = lax.axis_size(axis)
+    repeats = [devices if d == dim else 1 for d in range(x.ndim)]
+    return lax.all_to_all(jnp.tile(x, repeats), axis, split_axis=dim, concat_axis=dim, tiled=True)
 
 
 def from_everyone(array, axis):
@@ -126,9 +132,7 @@
     row_total = cond_act.shape[0]
     packed_width = packed.shape[1]
     mod_local = jnp.dot(
-        cond_act,
-        lax.all_gather(packed, "dp", axis=0, tiled=True),
-        preferred_element_type=jnp.float32,
+        cond_act, gather_from_all(packed, "dp", 0), preferred_element_type=jnp.float32
     )
     gathered = lax.all_gather(mod_local.astype(jnp.bfloat16), "tensor", axis=1, tiled=True).astype(
         mod_local.dtype

time: 164 us -> 225 us (1.37)
  the two profiles are of different devices: /device:TPU:1 before, /device:TPU:5 now
where the time goes in v1:
time: 225 us; the launch traced here: 224 us
  waiting for transfers between devices  137 us (61%)
  matrix products  23.3 us (10%)
  local copies, waits for them, and re-layouts  21.4 us (10%)
  other arithmetic  15.2 us (7%)
  blocking collectives  14.5 us (6%)
  starting transfers between devices  11.2 us (5%)
    all_to_all x1, waiting for transfers between devices, gather_from_all(): lax.all_to_all(jnp.tile(x, repeats), axis, split_axis=dim, concat_axis=di...  137 us
    all_to_all x2, blocking collectives, from_everyone(): lax.all_to_all(jnp.broadcast_to(array[None], (peers, *array.shape)), axis...  11.2 us
    all_to_all x1, starting transfers between devices, gather_from_all(): lax.all_to_all(jnp.tile(x, repeats), axis, split_axis=dim, concat_axis=di...  11.2 us
    dot_general x2, matrix products, evaluate(): jnp.einsum('ltd,dck->ltck', attn_in, qkv_weight[0], preferred_element_typ...  10.4 us
    all_to_all x1, local copies, waits for them, and re-layouts, gather_from_all(): lax.all_to_all(jnp.tile(x, repeats), axis, split_axis=dim, concat_axis=di...  10 us
    sub x2, other arithmetic, attend(): attn_probs = jax.nn.softmax(scores, axis=-1).astype(jnp.bfloat16)  6.48 us
    unnamed x35, local copies, waits for them, and re-layouts  5.79 us
  transfers between devices with their start and end apart: 1, of which 1 were waited for; matrix products, arithmetic and copies ran while one was open for 2% of the time, Pallas kernels for 0%

profile of v1, /device:TPU:5, one launch (start us, length us, event | category | flops | bytes accessed | tf_op | source)
XLA Modules:
  0.0 224.0 jit_solution(1841972504329356452)
XLA Ops:
  0.6 1.2 pad_maximum_fusion.1
  1.8 4.1 %tile.2 = bf16[64,18,2880]{2,1,0:T(8,128)(2,1)} broadcast(bf16[18,2880]{1,0:T(8,128)(2,1)S(1)} %pad_maximum_fusion.1), dimensions={1,2} | broadcast | bytes 6739200 | tf_op jit(solution)/shard_map/tile | solution.py:20
  5.9 11.2 %all-to-all-start = ((bf16[64,18,2880]{2,1,0:T(8,128)(2,1)}), bf16[64,18,2880]{2,1,0:T(8,128)(2,1)}, u32[]{:S(2)}, u32[]{:S(2)}) async-start(bf16[64,18,2880]{2,1,0:T(8,128)(2,1)} %tile.2), calls=%async_computation | async-start | bytes 18087936 | tf_op jit(solution)/shard_map/all_to_all | solution.py:20
  17.5 2.3 %multiply_sine_fusion = (f32[256,576]{1,0:T(8,128)S(1)}, f32[256,576]{1,0:T(8,128)S(1)}) fusion(f32[576]{0:T(1024)S(1)} %multiply_exponential_fusion, f32[256]{0:T(256)S(1)} %iota_convert_fusion), kind=kLoop, calls=%fused_computation.57 | loop fusion | flops 147456 | bytes 1182976 | tf_op jit(solution)/shard_map/sin | solution.py:56
  19.8 0.2 pad_maximum_fusion
  20.1 1.0 copy-done.4
  21.1 0.5 fusion.78
  21.7 1.4 copy-done.2
  23.0 0.4 multiply_reduce_fusion.5
  23.6 0.2 fusion.60
  23.8 137.3 %all-to-all-done = bf16[64,18,2880]{2,1,0:T(8,128)(2,1)} async-done(((bf16[64,18,2880]{2,1,0:T(8,128)(2,1)}), bf16[64,18,2880]{2,1,0:T(8,128)(2,1)}, u32[]{:S(2)}, u32[]{:S(2)}) %all-to-all-start) | async-done | bytes 6635552 | tf_op jit(solution)/shard_map/all_to_all | solution.py:20
  161.1 10.0 %all_to_all.13 = bf16[1152,2880]{1,0:T(8,128)(2,1)} reshape(bf16[64,18,2880]{2,1,0:T(8,128)(2,1)} %all-to-all-done) | data formatting | bytes 13271040 | tf_op jit(solution)/shard_map/all_to_all | solution.py:20
  171.1 4.3 %fusion.8 = bf16[1,2880,4]{1,2,0:T(4,128)(2,1)S(1)} fusion(bf16[1152,2880]{1,0:T(8,128)(2,1)} %all_to_all.13, bf16[1152,1152]{1,0:T(8,128)(2,1)S(1)} %copy-done, f32[4,1152]{1,0:T(4,128)S(1)} %fusion.60, bf16[2,1152]{1,0:T(2,128)(2,1)S(1)} %copy-done.9), kind=kOutput, calls=%fused_computation.19 | convolution fusion | flops 37239552 | bytes 9335808 | tf_op jit(solution)/shard_map/dot_general | solution.py:134
  175.4 3.2 %all-gather = bf16[2,2880,4]{1,2,0:T(4,128)(2,1)S(1)} all-gather(bf16[1,2880,4]{1,2,0:T(4,128)(2,1)S(1)} %fusion.8), channel_id=1, replica_groups=mesh['dp'=64,'tensor'=2] {'tensor'}, dimensions={0}, use_global_device_ids=true | all-gather | bytes 69120 | tf_op jit(solution)/shard_map/all_gather | solution.py:137
  178.7 0.1 reshape.173
  179.2 5.6 %fusion.17 = bf16[2,256,3,576]{1,3,2,0:T(8,128)(2,1)S(1)} fusion(bf16[1,1152,3,576]{1,3,2,0:T(8,128)(2,1)} %param.23, f32[2,256,1152]{2,1,0:T(8,128)} %copy-done.2, f32[2,1152]{1,0:T(2,128)S(1)} %get-tuple-element.21, f32[2,1152]{1,0:T(2,128)S(1)} %get-tuple-element.22, f32[2,256]{1,0:T(2,128)S(1)} %add_rsqrt_fusion.3, ...), kind=kOutput, calls=%fused_computation.37 | convolution fusion | flops 2042265600 | bytes 8132608 | tf_op jit(solution)/shard_map/ltd,dck->ltck/dot_general | solution.py:160
  184.8 0.8 fusion.42
  185.5 3.2 %fusion.79 = (f32[2,8,256]{2,1,0:T(8,128)S(1)}, f32[2,8,256,256]{2,3,1,0:T(8,128)S(1)}) fusion(f32[2,8,256,256]{2,3,1,0:T(8,128)S(1)} %fusion.42), kind=kOutput, calls=%fused_computation.139 | output fusion | flops 4194559 | bytes 8404992 | tf_op jit(solution)/shard_map/sub | solution.py:95
  188.8 0.5 fusion.26
  189.3 0.8 copy-done.12
  190.1 1.2 convolution_convert_fusion.2
  191.3 0.2 broadcast_in_dim.10
  191.5 5.7 %all_to_all.19 = bf16[2,2,256,1152]{3,2,1,0:T(8,128)(2,1)S(1)} all-to-all(bf16[2,2,256,1152]{3,2,1,0:T(8,128)(2,1)S(1)} %broadcast_in_dim.10), channel_id=1, replica_groups=mesh['dp'=64,'tensor'=2] {'tensor'}, dimensions={0} | all-to-all | bytes 4718592 | tf_op jit(solution)/shard_map/all_to_all | solution.py:25
  197.2 0.4 convert_reduce_fusion.1
  197.6 1.3 copy-done.3
  198.9 0.4 fusion.74
  199.3 0.4 multiply_reduce_fusion.4
  199.7 0.3 copy-done.14
  200.0 0.6 fusion.39
  200.6 0.2 reshape.163
  201.1 1.8 fusion.80
  202.9 0.4 multiply_reduce_fusion.3
  203.4 4.8 %fusion.20 = bf16[2,256,3,576]{1,3,2,0:T(8,128)(2,1)S(1)} fusion(bf16[1,1152,3,576]{1,3,2,0:T(8,128)(2,1)} %param.23, f32[2,256,1152]{2,1,0:T(8,128)S(1)} %get-tuple-element.43, f32[2,1152]{1,0:T(2,128)S(1)} %get-tuple-element.18, f32[2,1152]{1,0:T(2,128)S(1)} %get-tuple-element.19, f32[2,256]{1,0:T(2,128)S(1)} %add_rsqrt_fusion.1, ...), kind=kOutput, calls=%fused_computation.38 | convolution fusion | flops 2042265600 | bytes 8132608 | tf_op jit(solution)/shard_map/ltd,dck->ltck/dot_general | solution.py:160
  208.3 0.7 fusion.41
  209.0 3.2 %fusion.81 = (f32[2,8,256]{2,1,0:T(8,128)S(1)}, f32[2,8,256,256]{2,3,1,0:T(8,128)S(1)}) fusion(f32[2,8,256,256]{2,3,1,0:T(8,128)S(1)} %fusion.41), kind=kOutput, calls=%fused_computation.141 | output fusion | flops 4194559 | bytes 8404992 | tf_op jit(solution)/shard_map/sub | solution.py:95
  212.3 0.5 fusion.25
  212.8 0.8 copy-done.13
  213.6 1.2 convolution_convert_fusion.1
  214.8 0.2 broadcast_in_dim.11
  215.0 5.5 %all_to_all.20 = bf16[2,2,256,1152]{3,2,1,0:T(8,128)(2,1)S(1)} all-to-all(bf16[2,2,256,1152]{3,2,1,0:T(8,128)(2,1)S(1)} %broadcast_in_dim.11), channel_id=1, replica_groups=mesh['dp'=64,'tensor'=2] {'tensor'}, dimensions={0} | all-to-all | bytes 4718592 | tf_op jit(solution)/shard_map/all_to_all | solution.py:25
  220.5 0.4 convert_reduce_fusion
  220.9 0.4 fusion.72
  221.3 0.4 multiply_reduce_fusion.2
  221.7 0.6 fusion.40
  222.3 0.2 reshape.166
  222.5 0.3 multiply_reduce_fusion.6
  222.8 0.5 multiply_sqrt_fusion
  223.3 0.7 broadcast_select_fusion
  (58 shorter events, 1.3 us)
Async XLA Ops:
  0.6 170.5 %copy-start = (bf16[1152,1152]{1,0:T(8,128)(2,1)S(1)}, bf16[1152,1152]{1,0:T(8,128)(2,1)}, u32[]{:S(2)}) copy-start(bf16[1152,1152]{1,0:T(8,128)(2,1)} %param.22) | copy-start | bytes 7962628
  5.9 11.2 %copy-start.6 = (f32[2,4096]{1,0:T(2,128)S(1)}, f32[2,4096]{1,0:T(2,128)}, u32[]{:S(2)}) copy-start(f32[2,4096]{1,0:T(2,128)} %param.14) | copy-start | bytes 98308
  5.9 11.4 %copy-start.10 = (f32[2]{0:T(128)S(1)}, f32[2]{0:T(128)}, u32[]{:S(2)}) copy-start(f32[2]{0:T(128)} %param.18) | copy-start | bytes 28
  5.9 11.4 %copy-start.11 = (f32[2]{0:T(128)S(1)}, f32[2]{0:T(128)}, u32[]{:S(2)}) copy-start(f32[2]{0:T(128)} %param.17) | copy-start | bytes 28
  5.9 155.2 %all-to-all-start = ((bf16[64,18,2880]{2,1,0:T(8,128)(2,1)}), bf16[64,18,2880]{2,1,0:T(8,128)(2,1)}, u32[]{:S(2)}, u32[]{:S(2)}) async-start(bf16[64,18,2880]{2,1,0:T(8,128)(2,1)} %tile.2), calls=%async_computation | async-start | bytes 18087936 | tf_op jit(solution)/shard_map/all_to_all | solution.py:20
  17.1 4.0 %copy-start.7 = (bf16[16,1152]{1,0:T(8,128)(2,1)S(1)}, bf16[16,1152]{1,0:T(8,128)(2,1)}, u32[]{:S(2)}) copy-start(bf16[16,1152]{1,0:T(8,128)(2,1)} %param.20) | copy-start | bytes 110596
  20.1 1.0 copy-start.4
  21.1 2.3 %copy-start.15 = (s32[2]{0:T(128)S(1)}, s32[2]{0:T(128)}, u32[]{:S(2)}) copy-start(s32[2]{0:T(128)} %param.19) | copy-start | bytes 28
  21.1 2.5 %copy-start.5 = (bf16[256,1152]{1,0:T(8,128)(2,1)S(1)}, bf16[256,1152]{1,0:T(8,128)(2,1)}, u32[]{:S(2)}) copy-start(bf16[256,1152]{1,0:T(8,128)(2,1)} %param.21) | copy-start | bytes 1769476
  21.6 1.4 copy-start.2
  23.8 147.3 %copy-start.9 = (bf16[2,1152]{1,0:T(2,128)(2,1)S(1)}, bf16[2,1152]{1,0:T(2,128)(2,1)}, u32[]{:S(2)}) copy-start(bf16[2,1152]{1,0:T(2,128)(2,1)} %param.16) | copy-start | bytes 13828
  188.8 1.3 copy-start.12
  197.2 1.7 copy-start.3
  199.3 0.8 copy-start.14
  199.7 1.1 copy-start.8
  212.3 1.3 copy-start.13
  221.3 2.7 %copy-start.1 = (bf16[1152,1152]{1,0:T(8,128)(2,1)S(1)}, bf16[1152,1152]{1,0:T(8,128)(2,1)}, u32[]{:S(2)}) copy-start(bf16[1152,1152]{1,0:T(8,128)(2,1)} %param.22) | copy-start | bytes 7962628
